TPU v7x, 32 devices: a whole 2x2x4 slice. The times are simulated.
32 devices in a mesh: group: 2 (over y), ha: 4 (over x, core), wa: 4 (over z).
Axes of the slice: x: 2, y: 2, z: 4, core: 2. Of those that a mesh axis runs over, the one named last changes fastest.
Arguments:
- queries: bfloat16 [4, 32, 32, 1536], P('group', 'ha', 'wa'), parts along dimension 0, may hold values from -6 to 6
- keys: bfloat16 [4, 32, 32, 1536], P('group', 'ha', 'wa'), parts along dimension 0, may hold values from -6 to 6
- values: bfloat16 [4, 32, 32, 1536], P('group', 'ha', 'wa'), parts along dimension 0, may hold values from -6 to 6
- out_grad: bfloat16 [4, 32, 32, 1536], P('group', 'ha', 'wa'), parts along dimension 0, may hold values from -96 to 96
- log_norm: float32 [12, 4, 32, 32], P(None, 'group', 'ha', 'wa'), parts along dimension 1, may hold values from 6.5 to 7.5
- delta_rows: float32 [12, 4, 32, 32], P(None, 'group', 'ha', 'wa'), parts along dimension 1, may hold values from -360 to 360
- text_keys: bfloat16 [64, 1536], P('group'), parts along dimension 0, may hold values from -6 to 6
- text_values: bfloat16 [64, 1536], P('group'), parts along dimension 0, may hold values from -6 to 6
- window_table: int32 [4, 4, 9], replicated, may hold values 0 or 1
Outputs:
- query_grad: bfloat16 [4, 32, 32, 1536], P('group', 'ha', 'wa'), parts along dimension 0
- key_grad: bfloat16 [4, 32, 32, 1536], P('group', 'ha', 'wa'), parts along dimension 0
- value_grad: bfloat16 [4, 32, 32, 1536], P('group', 'ha', 'wa'), parts along dimension 0
- text_key_grad: bfloat16 [64, 1536], P('group'), parts along dimension 0
- text_value_grad: bfloat16 [64, 1536], P('group'), parts along dimension 0
There are 2 independent parts, one for each index of `group`. A program takes and returns all parts, laid end to end along the dimension named above; an argument that names none is the same for every part. Nothing has to cross between parts.
All inputs are finite; a program needn't handle non-finite values.
Results may differ from a plain program's by a relative error of at most 0.001.
The roundings to bfloat16 on the way count: a program that leaves them out, or rounds other values in their place, can miss the bound.
Values may be sent and summed in bfloat16 or wider, within the bound.
A program may use at most 64 MiB of HBM per device.

v0:
```python
import math
import jax
import jax.numpy as jnp
from jax import lax
from jax.sharding import PartitionSpec as P

HEADS = 12
HDIM = 128
TILE = 8
HALO = 2


def passed_along(value, axis, steps):
    count = lax.axis_size(axis)
    pairs = [(source, (source + steps) % count) for source in range(count)]
    return lax.ppermute(value, axis, pairs)


def with_halo(cells, sides, width):
    for axis, dim in sides:
        count = lax.axis_size(axis)
        head = lax.slice_in_dim(cells, 0, width, axis=dim)
        tail = lax.slice_in_dim(cells, cells.shape[dim] - width, cells.shape[dim], axis=dim)
        cells = jnp.concatenate(
            [
                lax.ppermute(tail, axis, [(i, (i + 1) % count) for i in range(count)]),
                cells,
                lax.ppermute(head, axis, [((i + 1) % count, i) for i in range(count)]),
            ],
            axis=dim,
        )
    return cells


def tile_grads(query_rows, cotangent_rows, norm_rows, delta_part, key_rows, value_rows, cell_mask):
    score_scale = 1.0 / math.sqrt(query_rows.shape[-1])
    scores = (
        jnp.einsum("qhd,khd->hqk", query_rows, key_rows, preferred_element_type=jnp.float32)
        * score_scale
    )
    probs = jnp.exp(scores - norm_rows[:, :, None])
    if cell_mask is not None:
        probs = probs * cell_mask[None, None, :]
    probs_half = probs.astype(jnp.bfloat16)
    value_part = jnp.einsum(
        "hqk,qhd->khd", probs_half, cotangent_rows, preferred_element_type=jnp.float32
    )
    prob_grad = jnp.einsum(
        "qhd,khd->hqk", cotangent_rows, value_rows, preferred_element_type=jnp.float32
    )
    score_grad = (probs * (prob_grad - delta_part[:, :, None])).astype(jnp.bfloat16)
    query_part = (
        jnp.einsum("hqk,khd->qhd", score_grad, key_rows, preferred_element_type=jnp.float32)
        * score_scale
    )
    key_part = (
        jnp.einsum("hqk,qhd->khd", score_grad, query_rows, preferred_element_type=jnp.float32)
        * score_scale
    )
    return (query_part, key_part, value_part)


def send_cols(strip, offset):
    return passed_along(strip, "wa", offset)


def send_rows(strip, offset):
    return passed_along(strip, "ha", offset)


def fold_band(buffer, along, mover):
    lower = lax.slice_in_dim(buffer, 0, HALO, axis=along)
    middle = lax.slice_in_dim(buffer, HALO, HALO + TILE, axis=along)
    upper = lax.slice_in_dim(buffer, HALO + TILE, TILE + 2 * HALO, axis=along)
    from_before = mover(upper, 1)
    from_after = mover(lower, -1)
    widths_low = [(0, 0)] * buffer.ndim
    widths_high = [(0, 0)] * buffer.ndim
    widths_low[along] = (0, TILE - HALO)
    widths_high[along] = (TILE - HALO, 0)
    return middle + jnp.pad(from_before, widths_low) + jnp.pad(from_after, widths_high)


def local(
    queries, keys, values, out_grad, log_norm, delta_rows, text_keys, text_values, window_table
):
    frames, tile_side, _, width = queries.shape
    window_side = TILE + 2 * HALO
    stacked = jnp.stack((keys, values))
    window = with_halo(stacked, (("ha", 2), ("wa", 3)), HALO)
    row_tile = lax.axis_index("ha")
    col_tile = lax.axis_index("wa")
    anchor = jnp.zeros((), jnp.int32)
    pattern = (
        lax.dynamic_slice(window_table, (row_tile, col_tile, anchor), (1, 1, 9))
        .reshape(3, 3)
        .astype(jnp.float32)
    )
    position = jnp.arange(window_side, dtype=jnp.int32)
    block_of = (position >= HALO).astype(jnp.int32) + (position >= HALO + TILE).astype(jnp.int32)
    one_hot = (block_of[:, None] == jnp.arange(3, dtype=jnp.int32)[None, :]).astype(jnp.float32)
    cell_grid = jnp.dot(
        jnp.dot(one_hot, pattern, precision=lax.Precision.HIGHEST),
        one_hot.T,
        precision=lax.Precision.HIGHEST,
    )
    cell_mask = jnp.broadcast_to(cell_grid[None], (frames, window_side, window_side)).reshape(-1)
    query_rows = queries.reshape(-1, HEADS, HDIM)
    cotangent_rows = out_grad.reshape(-1, HEADS, HDIM)
    norm_rows = log_norm.reshape(HEADS, -1)
    delta_part = delta_rows.reshape(HEADS, -1)
    key_rows = window[0].reshape(-1, HEADS, HDIM)
    value_rows = window[1].reshape(-1, HEADS, HDIM)
    video_query, video_key, video_value = tile_grads(
        query_rows, cotangent_rows, norm_rows, delta_part, key_rows, value_rows, cell_mask
    )
    text_query, text_key, text_value = tile_grads(
        query_rows,
        cotangent_rows,
        norm_rows,
        delta_part,
        text_keys.reshape(-1, HEADS, HDIM),
        text_values.reshape(-1, HEADS, HDIM),
        None,
    )
    query_grad = (
        (video_query + text_query).astype(jnp.bfloat16).reshape(frames, tile_side, tile_side, width)
    )
    text_total = lax.psum(jnp.stack((text_key, text_value)), ("ha", "wa"))
    buffer = jnp.stack((video_key, video_value)).reshape(2, frames, window_side, window_side, width)
    buffer = fold_band(buffer, 2, send_rows)
    buffer = fold_band(buffer, 3, send_cols)
    text_key_grad = text_total[0].reshape(-1, width).astype(jnp.bfloat16)
    text_value_grad = text_total[1].reshape(-1, width).astype(jnp.bfloat16)
    return (
        query_grad,
        buffer[0].astype(jnp.bfloat16),
        buffer[1].astype(jnp.bfloat16),
        text_key_grad,
        text_value_grad,
    )


def solution(mesh):
    in_specs = (
        P("group", "ha", "wa", None),
        P("group", "ha", "wa", None),
        P("group", "ha", "wa", None),
        P("group", "ha", "wa", None),
        P(None, "group", "ha", "wa"),
        P(None, "group", "ha", "wa"),
        P("group", None),
        P("group", None),
        P(),
    )
    out_specs = (
        P("group", "ha", "wa", None),
        P("group", "ha", "wa", None),
        P("group", "ha", "wa", None),
        P("group", None),
        P("group", None),
    )
    return jax.shard_map(local, mesh=mesh, in_specs=in_specs, out_specs=out_specs, check_vma=False)
```

profile of v0, /device:TPU:0, one launch (start us, length us, event | category | flops | bytes accessed | tf_op | source)
XLA Modules:
  0.0 151.5 jit_solution(18392472798687320180)
XLA Ops:
  0.7 1.1 pad_maximum_fusion.7
  1.8 0.5 collective-permute-start
  2.4 2.0 %collective-permute-start.1 = (bf16[2,2,2,8,1536]{4,3,2,1,0:T(8,128)(2,1)S(1)}, bf16[2,2,2,8,1536]{4,3,2,1,0:T(8,128)(2,1)S(1)}, u32[]{:S(2)}, u32[]{:S(2)}) collective-permute-start(bf16[2,2,2,8,1536]{4,3,2,1,0:T(8,128)(2,1)S(1)} %get-tuple-element.21), channel_id=1, source_target_pairs={{4,0},{8,4},{12,8},{0,12},{5,1},{9,5},{13,9},{1,13},{6,2},{10,6},{... | collective-permute-start | bytes 589832 | tf_op jit(solution)/shard_map/ppermute | solution.py:28
  4.3 0.7 convert_reduce_fusion
  5.5 0.9 copy.59
  6.4 0.9 copy.62
  7.4 1.4 reshape.49
  8.8 0.3 reshape.50
  9.0 0.3 fusion.10
  9.4 0.3 fusion.11
  9.7 0.7 copy-done.9
  10.4 0.2 fusion.7
  11.0 1.2 pad_maximum_fusion.5
  12.1 2.3 %collective-permute-start.2 = (bf16[2,2,12,2,1536]{4,3,2,1,0:T(2,128)(2,1)}, bf16[2,2,12,2,1536]{4,3,2,1,0:T(2,128)(2,1)S(1)}, u32[]{:S(2)}, u32[]{:S(2)}) collective-permute-start(bf16[2,2,12,2,1536]{4,3,2,1,0:T(2,128)(2,1)} %get-tuple-element.16), channel_id=1, source_target_pairs={{0,1},{1,2},{2,3},{3,0},{4,5},{5,6},{6,7},{7,4},{8,9},{9,10},{10,1... | collective-permute-start | bytes 884744 | tf_op jit(solution)/shard_map/ppermute | solution.py:26
  14.5 2.0 %collective-permute-start.3 = (bf16[2,2,12,2,1536]{4,3,2,1,0:T(2,128)(2,1)}, bf16[2,2,12,2,1536]{4,3,2,1,0:T(2,128)(2,1)S(1)}, u32[]{:S(2)}, u32[]{:S(2)}) collective-permute-start(bf16[2,2,12,2,1536]{4,3,2,1,0:T(2,128)(2,1)} %get-tuple-element.17), channel_id=1, source_target_pairs={{1,0},{2,1},{3,2},{0,3},{5,4},{6,5},{7,6},{4,7},{9,8},{10,9},{11,1... | collective-permute-start | bytes 884744 | tf_op jit(solution)/shard_map/ppermute | solution.py:28
  16.5 73.5 %all-reduce.5 = bf16[2,32,12,128]{3,1,2,0:T(8,128)(2,1)} all-reduce(f32[2,32,12,128]{3,1,2,0:T(8,128)S(1)} %pad_maximum_fusion.1), channel_id=1, replica_groups=mesh['group'=2,'ha'=4,'wa'=4] {'ha','wa'}, use_global_device_ids=true, to_apply=%region_0.0 | all-reduce | flops 98304 | bytes 589824 | tf_op jit(solution)/shard_map/psum | solution.py:129
  90.0 1.5 pad_maximum_fusion
  91.7 1.7 %reshape_squeeze.9 = bf16[288,12,128]{2,1,0:T(8,128)(2,1)} reshape(bf16[1,2,12,12,1536]{4,3,2,1,0:T(8,128)(2,1)S(1)} %get-tuple-element.14) | data formatting | bytes 1769472 | tf_op jit(solution)/shard_map/reshape;squeeze | solution.py:113
  93.3 0.8 reshape_squeeze.8
  94.2 0.6 exponential_multiply_fusion
  94.7 1.6 %convolution_bitcast_fusion = f32[288,12,128]{2,0,1:T(8,128)} fusion(f32[12,288,128]{2,1,0:T(8,128)S(1)} %exponential_multiply_fusion, bf16[128,12,128]{2,1,0:T(8,128)(2,1)S(1)} %reshape.50), kind=kOutput, calls=%fused_computation.9 | convolution fusion | flops 113688576 | bytes 3932160 | tf_op jit(solution)/shard_map/hqk,qhd->khd/dot_general | solution.py:45
  96.4 0.5 multiply_convert_fusion
  96.9 0.4 multiply_bitcast_fusion
  97.2 0.5 copy-done.2
  97.8 2.5 %copy.75 = f32[288,12,128]{2,1,0:T(8,128)} copy(f32[288,12,128]{2,0,1:T(8,128)S(1)} %multiply_bitcast_fusion) | data formatting | bytes 3538944 | tf_op jit(solution)/shard_map/mul | solution.py:57
  100.3 2.4 %stack.30 = f32[1,2,12,12,1536]{4,3,2,1,0:T(8,128)S(1)} reshape(f32[288,12,128]{2,1,0:T(8,128)} %copy.75) | data formatting | bytes 3538944 | tf_op jit(solution)/shard_map/stack | solution.py:130
  102.7 4.0 %copy.77 = f32[288,12,128]{2,1,0:T(8,128)} copy(f32[288,12,128]{2,0,1:T(8,128)} %convolution_bitcast_fusion) | data formatting | bytes 3538944 | tf_op jit(solution)/shard_map/hqk,qhd->khd/transpose | solution.py:45
  106.6 3.2 %stack.31 = f32[1,2,12,12,1536]{4,3,2,1,0:T(8,128)} reshape(f32[288,12,128]{2,1,0:T(8,128)} %copy.77) | data formatting | bytes 3538944 | tf_op jit(solution)/shard_map/stack | solution.py:130
  109.8 0.2 constant_dynamic-update-slice_fusion.1
  110.1 1.4 copy-done.1
  111.5 0.2 constant_dynamic-update-slice_fusion
  111.9 0.5 copy.78
  112.4 0.5 copy.80
  112.9 0.5 collective-permute-start.4
  113.5 0.7 copy_bitcast_fusion
  114.2 12.1 %collective-permute-done.5 = f32[2,2,2,12,1536]{4,2,3,1,0:T(2,128)S(1)} collective-permute-done((f32[2,2,2,12,1536]{4,2,3,1,0:T(2,128)S(1)}, f32[2,2,2,12,1536]{4,2,3,1,0:T(2,128)S(1)}, u32[]{:S(2)}, u32[]{:S(2)}) %collective-permute-start.5) | collective-permute-done | bytes 589856 | tf_op jit(solution)/shard_map/ppermute | solution.py:16
  126.4 1.4 collective-permute-done.4
  128.0 0.4 fusion
  128.4 1.2 fusion.37
  129.6 3.8 %collective-permute-start.7 = (f32[2,2,8,2,1536]{4,3,2,1,0:T(2,128)}, f32[2,2,8,2,1536]{4,3,2,1,0:T(2,128)}, u32[]{:S(2)}, u32[]{:S(2)}) collective-permute-start(f32[2,2,8,2,1536]{4,3,2,1,0:T(2,128)} %get-tuple-element.13), channel_id=1, source_target_pairs={{0,3},{1,0},{2,1},{3,2},{4,7},{5,4},{6,5},{7,6},{8,11},{9,8},{10,9... | collective-permute-start | bytes 1179656 | tf_op jit(solution)/shard_map/ppermute | solution.py:16
  133.5 0.6 fusion.5
  134.1 1.1 fusion.6
  135.1 2.2 %copy.73 = bf16[128,12,128]{2,1,0:T(8,128)(2,1)} copy(bf16[128,12,128]{0,2,1:T(8,128)(2,1)} %fusion.6) | data formatting | bytes 786432 | tf_op jit(solution)/shard_map/convert_element_type | solution.py:127
  137.3 2.1 %reshape.53 = bf16[2,8,8,1536]{3,2,1,0:T(8,128)(2,1)} reshape(bf16[128,12,128]{2,1,0:T(8,128)(2,1)} %copy.73) | data formatting | bytes 786432 | tf_op jit(solution)/shard_map/reshape | solution.py:127
  139.4 4.4 %collective-permute-done.6 = f32[2,2,8,2,1536]{4,3,2,1,0:T(2,128)} collective-permute-done((f32[2,2,8,2,1536]{4,3,2,1,0:T(2,128)}, f32[2,2,8,2,1536]{4,3,2,1,0:T(2,128)}, u32[]{:S(2)}, u32[]{:S(2)}) %collective-permute-start.6) | collective-permute-done | bytes 393248 | tf_op jit(solution)/shard_map/ppermute | solution.py:16
  143.7 5.2 %collective-permute-done.7 = f32[2,2,8,2,1536]{4,3,2,1,0:T(2,128)} collective-permute-done((f32[2,2,8,2,1536]{4,3,2,1,0:T(2,128)}, f32[2,2,8,2,1536]{4,3,2,1,0:T(2,128)}, u32[]{:S(2)}, u32[]{:S(2)}) %collective-permute-start.7) | collective-permute-done | bytes 393248 | tf_op jit(solution)/shard_map/ppermute | solution.py:16
  149.0 1.6 %fusion.2 = bf16[2,2,8,8,1536]{4,3,2,1,0:T(8,128)(2,1)S(1)} fusion(f32[2,2,8,12,1536]{4,3,2,1,0:T(8,128)S(1)} %fusion, f32[2,2,8,2,1536]{4,3,2,1,0:T(2,128)} %collective-permute-done.7, f32[2,2,8,2,1536]{4,3,2,1,0:T(2,128)} %collective-permute-done.6), kind=kLoop, calls=%fused_computation.8 | loop fusion | flops 1179648 | bytes 3145728 | tf_op jit(solution)/shard_map/convert.3
  150.5 0.9 slice_bitcast_fusion
  (46 shorter events, 1.6 us)
Async XLA Ops:
  0.6 8.4 %copy-start = (bf16[32,1536]{1,0:T(8,128)(2,1)S(1)}, bf16[32,1536]{1,0:T(8,128)(2,1)}, u32[]{:S(2)}) copy-start(bf16[32,1536]{1,0:T(8,128)(2,1)} %param.15) | copy-start | bytes 294916
  0.6 8.1 %copy-start.12 = (bf16[2,8,8,1536]{3,2,1,0:T(8,128)(2,1)S(1)}, bf16[2,8,8,1536]{3,2,1,0:T(8,128)(2,1)}, u32[]{:S(2)}) copy-start(bf16[2,8,8,1536]{3,2,1,0:T(8,128)(2,1)} %param.12) | copy-start | bytes 1179652
  0.7 8.7 %copy-start.13 = (bf16[32,1536]{1,0:T(8,128)(2,1)S(1)}, bf16[32,1536]{1,0:T(8,128)(2,1)}, u32[]{:S(2)}) copy-start(bf16[32,1536]{1,0:T(8,128)(2,1)} %param.16) | copy-start | bytes 294916
  1.8 9.1 %collective-permute-start = (bf16[2,2,2,8,1536]{4,3,2,1,0:T(8,128)(2,1)S(1)}, bf16[2,2,2,8,1536]{4,3,2,1,0:T(8,128)(2,1)S(1)}, u32[]{:S(2)}, u32[]{:S(2)}) collective-permute-start(bf16[2,2,2,8,1536]{4,3,2,1,0:T(8,128)(2,1)S(1)} %get-tuple-element.20), channel_id=1, source_target_pairs={{0,4},{4,8},{8,12},{12,0},{1,5},{5,9},{9,13},{13,1},{2,6},{6,10},{... | collective-permute-start | bytes 589832 | tf_op jit(solution)/shard_map/ppermute | solution.py:26
  2.4 8.6 %collective-permute-start.1 = (bf16[2,2,2,8,1536]{4,3,2,1,0:T(8,128)(2,1)S(1)}, bf16[2,2,2,8,1536]{4,3,2,1,0:T(8,128)(2,1)S(1)}, u32[]{:S(2)}, u32[]{:S(2)}) collective-permute-start(bf16[2,2,2,8,1536]{4,3,2,1,0:T(8,128)(2,1)S(1)} %get-tuple-element.21), channel_id=1, source_target_pairs={{4,0},{8,4},{12,8},{0,12},{5,1},{9,5},{13,9},{1,13},{6,2},{10,6},{... | collective-permute-start | bytes 589832 | tf_op jit(solution)/shard_map/ppermute | solution.py:28
  7.4 3.6 %copy-start.7 = (bf16[2,8,8,1536]{3,2,1,0:T(8,128)(2,1)S(1)}, bf16[2,8,8,1536]{3,2,1,0:T(8,128)(2,1)}, u32[]{:S(2)}) copy-start(bf16[2,8,8,1536]{3,2,1,0:T(8,128)(2,1)} %param.11) | copy-start | bytes 1179652
  7.4 3.6 %copy-start.8 = (bf16[2,8,8,1536]{3,2,1,0:T(8,128)(2,1)S(1)}, bf16[2,8,8,1536]{3,2,1,0:T(8,128)(2,1)}, u32[]{:S(2)}) copy-start(bf16[2,8,8,1536]{3,2,1,0:T(8,128)(2,1)} %param.10) | copy-start | bytes 1179652
  9.7 0.7 copy-start.9
  12.1 77.9 %collective-permute-start.2 = (bf16[2,2,12,2,1536]{4,3,2,1,0:T(2,128)(2,1)}, bf16[2,2,12,2,1536]{4,3,2,1,0:T(2,128)(2,1)S(1)}, u32[]{:S(2)}, u32[]{:S(2)}) collective-permute-start(bf16[2,2,12,2,1536]{4,3,2,1,0:T(2,128)(2,1)} %get-tuple-element.16), channel_id=1, source_target_pairs={{0,1},{1,2},{2,3},{3,0},{4,5},{5,6},{6,7},{7,4},{8,9},{9,10},{10,1... | collective-permute-start | bytes 884744 | tf_op jit(solution)/shard_map/ppermute | solution.py:26
  14.5 75.5 %collective-permute-start.3 = (bf16[2,2,12,2,1536]{4,3,2,1,0:T(2,128)(2,1)}, bf16[2,2,12,2,1536]{4,3,2,1,0:T(2,128)(2,1)S(1)}, u32[]{:S(2)}, u32[]{:S(2)}) collective-permute-start(bf16[2,2,12,2,1536]{4,3,2,1,0:T(2,128)(2,1)} %get-tuple-element.17), channel_id=1, source_target_pairs={{1,0},{2,1},{3,2},{0,3},{5,4},{6,5},{7,6},{4,7},{9,8},{10,9},{11,1... | collective-permute-start | bytes 884744 | tf_op jit(solution)/shard_map/ppermute | solution.py:28
  94.1 2.2 %copy-start.4 = (bf16[288,12,128]{2,1,0:T(8,128)(2,1)}, bf16[288,12,128]{2,1,0:T(8,128)(2,1)S(1)}, u32[]{:S(2)}) copy-start(bf16[288,12,128]{2,1,0:T(8,128)(2,1)S(1)} %reshape_squeeze.8) | copy-start | bytes 2654212
  94.7 1.6 %copy-start.6 = (bf16[288,12,128]{2,1,0:T(8,128)(2,1)S(1)}, bf16[288,12,128]{2,1,0:T(8,128)(2,1)}, u32[]{:S(2)}) copy-start(bf16[288,12,128]{2,1,0:T(8,128)(2,1)} %reshape_squeeze.9) | copy-start | bytes 2654212
  96.8 0.9 copy-start.2
  109.8 1.7 %copy-start.1 = (f32[1,2,12,12,1536]{4,3,2,1,0:T(8,128)S(1)}, f32[1,2,12,12,1536]{4,3,2,1,0:T(8,128)}, u32[]{:S(2)}) copy-start(f32[1,2,12,12,1536]{4,3,2,1,0:T(8,128)} %stack.31) | copy-start | bytes 5308420
  111.7 1.6 %copy-start.11 = (bf16[2,32,12,128]{3,1,2,0:T(8,128)(2,1)S(1)}, bf16[2,32,12,128]{3,1,2,0:T(8,128)(2,1)}, u32[]{:S(2)}) copy-start(bf16[2,32,12,128]{3,1,2,0:T(8,128)(2,1)} %all-reduce.5) | copy-start | bytes 589828
  112.8 13.5 %collective-permute-start.5 = (f32[2,2,2,12,1536]{4,2,3,1,0:T(2,128)S(1)}, f32[2,2,2,12,1536]{4,2,3,1,0:T(2,128)S(1)}, u32[]{:S(2)}, u32[]{:S(2)}) collective-permute-start(f32[2,2,2,12,1536]{4,2,3,1,0:T(2,128)S(1)} %copy.80), channel_id=1, source_target_pairs={{0,12},{4,0},{8,4},{12,8},{1,13},{5,1},{9,5},{13,9},{2,14},{6,2},{... | collective-permute-start | bytes 1769480 | tf_op jit(solution)/shard_map/ppermute | solution.py:16
  112.9 15.0 %collective-permute-start.4 = (f32[2,2,2,12,1536]{4,2,3,1,0:T(2,128)S(1)}, f32[2,2,2,12,1536]{4,2,3,1,0:T(2,128)S(1)}, u32[]{:S(2)}, u32[]{:S(2)}) collective-permute-start(f32[2,2,2,12,1536]{4,2,3,1,0:T(2,128)S(1)} %copy.78), channel_id=1, source_target_pairs={{0,4},{4,8},{8,12},{12,0},{1,5},{5,9},{9,13},{13,1},{2,6},{6,10},{... | collective-permute-start | bytes 1769480 | tf_op jit(solution)/shard_map/ppermute | solution.py:16
  128.0 5.5 %copy-start.3 = (bf16[12,288,128]{2,1,0:T(8,128)(2,1)S(1)}, bf16[12,288,128]{2,1,0:T(8,128)(2,1)}, u32[]{:S(2)}) copy-start(bf16[12,288,128]{2,1,0:T(8,128)(2,1)} %copy-done.2) | copy-start | bytes 2654212
  128.0 5.4 %copy-start.5 = (bf16[288,12,128]{2,1,0:T(8,128)(2,1)S(1)}, bf16[288,12,128]{2,1,0:T(8,128)(2,1)}, u32[]{:S(2)}) copy-start(bf16[288,12,128]{2,1,0:T(8,128)(2,1)} %copy-done.4) | copy-start | bytes 2654212
  128.4 5.6 %copy-start.10 = (bf16[12,128,32]{1,2,0:T(8,128)(2,1)S(1)}, bf16[12,128,32]{1,2,0:T(8,128)(2,1)}, u32[]{:S(2)}) copy-start(bf16[12,128,32]{1,2,0:T(8,128)(2,1)} %copy-done.9) | copy-start | bytes 294916
  129.6 14.1 %collective-permute-start.6 = (f32[2,2,8,2,1536]{4,3,2,1,0:T(2,128)}, f32[2,2,8,2,1536]{4,3,2,1,0:T(2,128)}, u32[]{:S(2)}, u32[]{:S(2)}) collective-permute-start(f32[2,2,8,2,1536]{4,3,2,1,0:T(2,128)} %get-tuple-element.12), channel_id=1, source_target_pairs={{0,1},{1,2},{2,3},{3,0},{4,5},{5,6},{6,7},{7,4},{8,9},{9,10},{10,1... | collective-permute-start | bytes 1179656 | tf_op jit(solution)/shard_map/ppermute | solution.py:16
  129.6 19.3 %collective-permute-start.7 = (f32[2,2,8,2,1536]{4,3,2,1,0:T(2,128)}, f32[2,2,8,2,1536]{4,3,2,1,0:T(2,128)}, u32[]{:S(2)}, u32[]{:S(2)}) collective-permute-start(f32[2,2,8,2,1536]{4,3,2,1,0:T(2,128)} %get-tuple-element.13), channel_id=1, source_target_pairs={{0,3},{1,0},{2,1},{3,2},{4,7},{5,4},{6,5},{7,6},{8,11},{9,8},{10,9... | collective-permute-start | bytes 1179656 | tf_op jit(solution)/shard_map/ppermute | solution.py:16
where the time goes:
time: 152 us; the launch traced here: 151 us
  blocking collectives  73.5 us (48%)
  local copies, waits for them, and re-layouts  30 us (20%)
  waiting for transfers between devices  23.1 us (15%)
  starting transfers between devices  11.3 us (7%)
  other arithmetic  6.52 us (4%)
  matrix products  6.17 us (4%)
    psum x1, blocking collectives, local(): text_total = lax.psum(jnp.stack((text_key, text_value)), ('ha', 'wa'))  73.5 us
    ppermute x4, waiting for transfers between devices, passed_along(): return lax.ppermute(value, axis, pairs)  23.1 us
    another operation x3, local copies, waits for them, and re-layouts, local(): jnp.stack((video_key, video_value))  5.81 us
    ppermute x4, starting transfers between devices, passed_along(): return lax.ppermute(value, axis, pairs)  4.38 us
    ppermute x2, starting transfers between devices, with_halo(): lax.ppermute(head, axis, [((i + 1) % count, i) for i in range(count)])  4.01 us
    transpose x1, local copies, waits for them, and re-layouts, tile_grads(): jnp.einsum('hqk,qhd->khd', probs_half, cotangent_rows, preferred_element_...  3.98 us
  transfers between devices with their start and end apart: 8, of which 4 were waited for; matrix products, arithmetic and copies ran while one was open for 8% of the time, Pallas kernels for 0%

commit v1 on v0

--- a/solution.py
+++ b/solution.py
@@ -126,7 +126,7 @@
     query_grad = (
         (video_query + text_query).astype(jnp.bfloat16).reshape(frames, tile_side, tile_side, width)
     )
-    text_total = lax.psum(jnp.stack((text_key, text_value)), ("ha", "wa"))
+    text_total = lax.psum(lax.psum(jnp.stack((text_key, text_value)), "wa"), "ha")
     buffer = jnp.stack((video_key, video_value)).reshape(2, frames, window_side, window_side, width)
     buffer = fold_band(buffer, 2, send_rows)
     buffer = fold_band(buffer, 3, send_cols)

time: 152 us -> 149 us (0.980)
  blocking collectives: 73.5 us -> 15.5 us
  waiting for transfers between devices: 23.1 us -> 64.2 us
  between operations: 0.96 us -> 14.4 us
    psum x1, blocking collectives: 73.5 us -> 15.5 us  [local(): lax.psum(lax.psum(jnp.stack((text_key, text_value)), 'wa'), 'ha')]
    psum x0 -> x1, waiting for transfers between devices: none -> 38.4 us  [local(): lax.psum(jnp.stack((text_key, text_value)), 'wa')]
    ppermute x4, waiting for transfers between devices: 23.1 us -> 25.8 us  [passed_along(): return lax.ppermute(value, axis, pairs)]
  transfers between devices with their start and end apart: 8 -> 9, of which waited for: 4 -> 5; matrix products, arithmetic and copies ran while one was open for 8% -> 9% of each run, Pallas kernels for 0% -> 0%
where the time goes in v1:
time: 149 us; the launch traced here: 148 us
  waiting for transfers between devices  64.2 us (43%)
  local copies, waits for them, and re-layouts  29.9 us (20%)
  blocking collectives  15.5 us (10%)
  between operations  14.4 us (10%)
  starting transfers between devices  11.4 us (8%)
  other arithmetic  6.48 us (4%)
  matrix products  6.19 us (4%)
    psum x1, waiting for transfers between devices, local(): lax.psum(jnp.stack((text_key, text_value)), 'wa')  38.4 us
    ppermute x4, waiting for transfers between devices, passed_along(): return lax.ppermute(value, axis, pairs)  25.8 us
    psum x1, blocking collectives, local(): lax.psum(lax.psum(jnp.stack((text_key, text_value)), 'wa'), 'ha')  15.5 us
    another operation x3, local copies, waits for them, and re-layouts, local(): jnp.stack((video_key, video_value))  5.81 us
    ppermute x4, starting transfers between devices, passed_along(): return lax.ppermute(value, axis, pairs)  4.38 us
    ppermute x2, starting transfers between devices, with_halo(): lax.ppermute(head, axis, [((i + 1) % count, i) for i in range(count)])  4.07 us
    transpose x1, local copies, waits for them, and re-layouts, tile_grads(): jnp.einsum('hqk,qhd->khd', probs_half, cotangent_rows, preferred_element_...  3.98 us
  transfers between devices with their start and end apart: 9, of which 5 were waited for; matrix products, arithmetic and copies ran while one was open for 9% of the time, Pallas kernels for 0%

profile of v1, /device:TPU:0, one launch (start us, length us, event | category | flops | bytes accessed | tf_op | source)
XLA Modules:
  0.0 148.1 jit_solution(8815221435813066326)
XLA Ops:
  7.2 1.2 pad_maximum_fusion.7
  8.4 0.5 collective-permute-start
  9.0 2.0 %collective-permute-start.1 = (bf16[2,2,2,8,1536]{4,3,2,1,0:T(8,128)(2,1)S(1)}, bf16[2,2,2,8,1536]{4,3,2,1,0:T(8,128)(2,1)S(1)}, u32[]{:S(2)}, u32[]{:S(2)}) collective-permute-start(bf16[2,2,2,8,1536]{4,3,2,1,0:T(8,128)(2,1)S(1)} %get-tuple-element.21), channel_id=1, source_target_pairs={{4,0},{8,4},{12,8},{0,12},{5,1},{9,5},{13,9},{1,13},{6,2},{10,6},{... | collective-permute-start | bytes 589832 | tf_op jit(solution)/shard_map/ppermute | solution.py:28
  10.9 0.9 copy.59
  11.8 0.9 copy.62
  12.8 1.3 reshape.49
  14.1 0.3 reshape.50
  14.4 0.3 fusion.10
  14.9 0.3 fusion.11
  15.3 0.7 copy-done.9
  16.1 0.8 pad_maximum_fusion.1
  17.0 0.7 convert_reduce_fusion
  18.3 0.4 pad_maximum_fusion.5
  18.7 2.4 %collective-permute-start.2 = (bf16[2,2,12,2,1536]{4,3,2,1,0:T(2,128)(2,1)S(1)}, bf16[2,2,12,2,1536]{4,3,2,1,0:T(2,128)(2,1)S(1)}, u32[]{:S(2)}, u32[]{:S(2)}) collective-permute-start(bf16[2,2,12,2,1536]{4,3,2,1,0:T(2,128)(2,1)S(1)} %get-tuple-element.16), channel_id=1, source_target_pairs={{0,1},{1,2},{2,3},{3,0},{4,5},{5,6},{6,7},{7,4},{8,9},{9,10},{10,1... | collective-permute-start | bytes 884744 | tf_op jit(solution)/shard_map/ppermute | solution.py:26
  21.1 2.1 %collective-permute-start.3 = (bf16[2,2,12,2,1536]{4,3,2,1,0:T(2,128)(2,1)S(1)}, bf16[2,2,12,2,1536]{4,3,2,1,0:T(2,128)(2,1)S(1)}, u32[]{:S(2)}, u32[]{:S(2)}) collective-permute-start(bf16[2,2,12,2,1536]{4,3,2,1,0:T(2,128)(2,1)S(1)} %get-tuple-element.17), channel_id=1, source_target_pairs={{1,0},{2,1},{3,2},{0,3},{5,4},{6,5},{7,6},{4,7},{9,8},{10,9},{11,1... | collective-permute-start | bytes 884744 | tf_op jit(solution)/shard_map/ppermute | solution.py:28
  23.2 38.4 %all-reduce.7.cloned.1.call-done = f32[2,32,12,128]{3,1,2,0:T(8,128)} async-done(((f32[2,32,12,128]{3,1,2,0:T(8,128)}), f32[2,32,12,128]{3,1,2,0:T(8,128)}) %all-reduce.7.cloned.1.call-update) | async-done | bytes 393232 | tf_op jit(solution)/shard_map/psum | solution.py:129
  61.6 15.5 %all-reduce.8 = bf16[2,32,12,128]{3,1,2,0:T(8,128)(2,1)} all-reduce(f32[2,32,12,128]{3,1,2,0:T(8,128)} %all-reduce.7.cloned.1.call-done), channel_id=1, replica_groups=mesh['group'=2,'ha'=4,'wa'=4] {'ha'}, use_global_device_ids=true, to_apply=%region_1.0 | all-reduce | flops 98304 | bytes 589824 | tf_op jit(solution)/shard_map/psum | solution.py:129
  77.1 1.5 pad_maximum_fusion
  78.7 1.7 %reshape_squeeze.9 = bf16[288,12,128]{2,1,0:T(8,128)(2,1)} reshape(bf16[1,2,12,12,1536]{4,3,2,1,0:T(8,128)(2,1)S(1)} %get-tuple-element.14) | data formatting | bytes 1769472 | tf_op jit(solution)/shard_map/reshape;squeeze | solution.py:113
  80.4 0.8 reshape_squeeze.8
  81.2 0.6 exponential_multiply_fusion
  81.8 1.6 %convolution_bitcast_fusion = f32[288,12,128]{2,0,1:T(8,128)} fusion(f32[12,288,128]{2,1,0:T(8,128)S(1)} %exponential_multiply_fusion, bf16[128,12,128]{2,1,0:T(8,128)(2,1)S(1)} %reshape.50), kind=kOutput, calls=%fused_computation.9 | convolution fusion | flops 113688576 | bytes 3932160 | tf_op jit(solution)/shard_map/hqk,qhd->khd/dot_general | solution.py:45
  83.4 0.5 multiply_convert_fusion
  83.9 0.4 multiply_bitcast_fusion
  84.3 0.5 copy-done.2
  84.8 2.5 %copy.75 = f32[288,12,128]{2,1,0:T(8,128)} copy(f32[288,12,128]{2,0,1:T(8,128)S(1)} %multiply_bitcast_fusion) | data formatting | bytes 3538944 | tf_op jit(solution)/shard_map/mul | solution.py:57
  87.3 2.4 %stack.30 = f32[1,2,12,12,1536]{4,3,2,1,0:T(8,128)S(1)} reshape(f32[288,12,128]{2,1,0:T(8,128)} %copy.75) | data formatting | bytes 3538944 | tf_op jit(solution)/shard_map/stack | solution.py:130
  89.7 4.0 %copy.77 = f32[288,12,128]{2,1,0:T(8,128)} copy(f32[288,12,128]{2,0,1:T(8,128)} %convolution_bitcast_fusion) | data formatting | bytes 3538944 | tf_op jit(solution)/shard_map/hqk,qhd->khd/transpose | solution.py:45
  93.7 3.2 %stack.31 = f32[1,2,12,12,1536]{4,3,2,1,0:T(8,128)} reshape(f32[288,12,128]{2,1,0:T(8,128)} %copy.77) | data formatting | bytes 3538944 | tf_op jit(solution)/shard_map/stack | solution.py:130
  97.1 1.4 copy-done.1
  98.9 0.5 copy.78
  99.4 0.5 copy.80
  99.9 0.5 collective-permute-start.4
  100.5 0.7 copy_bitcast_fusion
  101.3 11.2 %collective-permute-done.5 = f32[2,2,2,12,1536]{4,2,3,1,0:T(2,128)S(1)} collective-permute-done((f32[2,2,2,12,1536]{4,2,3,1,0:T(2,128)S(1)}, f32[2,2,2,12,1536]{4,2,3,1,0:T(2,128)S(1)}, u32[]{:S(2)}, u32[]{:S(2)}) %collective-permute-start.5) | collective-permute-done | bytes 589856 | tf_op jit(solution)/shard_map/ppermute | solution.py:16
  112.6 3.1 %collective-permute-done.4 = f32[2,2,2,12,1536]{4,2,3,1,0:T(2,128)S(1)} collective-permute-done((f32[2,2,2,12,1536]{4,2,3,1,0:T(2,128)S(1)}, f32[2,2,2,12,1536]{4,2,3,1,0:T(2,128)S(1)}, u32[]{:S(2)}, u32[]{:S(2)}) %collective-permute-start.4) | collective-permute-done | bytes 589856 | tf_op jit(solution)/shard_map/ppermute | solution.py:16
  115.9 0.4 fusion
  116.3 1.2 fusion.37
  117.5 1.5 collective-permute-start.6
  119.0 2.4 %collective-permute-start.7 = (f32[2,2,8,2,1536]{4,3,2,1,0:T(2,128)}, f32[2,2,8,2,1536]{4,3,2,1,0:T(2,128)}, u32[]{:S(2)}, u32[]{:S(2)}) collective-permute-start(f32[2,2,8,2,1536]{4,3,2,1,0:T(2,128)} %get-tuple-element.13), channel_id=1, source_target_pairs={{0,3},{1,0},{2,1},{3,2},{4,7},{5,4},{6,5},{7,6},{8,11},{9,8},{10,9... | collective-permute-start | bytes 1179656 | tf_op jit(solution)/shard_map/ppermute | solution.py:16
  121.3 0.6 fusion.5
  121.9 1.1 fusion.6
  123.0 2.2 %copy.73 = bf16[128,12,128]{2,1,0:T(8,128)(2,1)} copy(bf16[128,12,128]{0,2,1:T(8,128)(2,1)} %fusion.6) | data formatting | bytes 786432 | tf_op jit(solution)/shard_map/convert_element_type | solution.py:127
  125.2 2.1 %reshape.53 = bf16[2,8,8,1536]{3,2,1,0:T(8,128)(2,1)} reshape(bf16[128,12,128]{2,1,0:T(8,128)(2,1)} %copy.73) | data formatting | bytes 786432 | tf_op jit(solution)/shard_map/reshape | solution.py:127
  127.2 4.4 %collective-permute-done.6 = f32[2,2,8,2,1536]{4,3,2,1,0:T(2,128)} collective-permute-done((f32[2,2,8,2,1536]{4,3,2,1,0:T(2,128)}, f32[2,2,8,2,1536]{4,3,2,1,0:T(2,128)}, u32[]{:S(2)}, u32[]{:S(2)}) %collective-permute-start.6) | collective-permute-done | bytes 393248 | tf_op jit(solution)/shard_map/ppermute | solution.py:16
  131.6 7.1 %collective-permute-done.7 = f32[2,2,8,2,1536]{4,3,2,1,0:T(2,128)} collective-permute-done((f32[2,2,8,2,1536]{4,3,2,1,0:T(2,128)}, f32[2,2,8,2,1536]{4,3,2,1,0:T(2,128)}, u32[]{:S(2)}, u32[]{:S(2)}) %collective-permute-start.7) | collective-permute-done | bytes 393248 | tf_op jit(solution)/shard_map/ppermute | solution.py:16
  138.7 1.6 %fusion.2 = bf16[2,2,8,8,1536]{4,3,2,1,0:T(8,128)(2,1)S(1)} fusion(f32[2,2,8,12,1536]{4,3,2,1,0:T(8,128)S(1)} %fusion, f32[2,2,8,2,1536]{4,3,2,1,0:T(2,128)} %collective-permute-done.7, f32[2,2,8,2,1536]{4,3,2,1,0:T(2,128)} %collective-permute-done.6), kind=kLoop, calls=%fused_computation.8 | loop fusion | flops 1179648 | bytes 3145728 | tf_op jit(solution)/shard_map/convert.3
  140.3 0.9 slice_bitcast_fusion
  (49 shorter events, 2.3 us)
Async XLA Ops:
  7.2 7.2 %copy-start = (bf16[32,1536]{1,0:T(8,128)(2,1)S(1)}, bf16[32,1536]{1,0:T(8,128)(2,1)}, u32[]{:S(2)}) copy-start(bf16[32,1536]{1,0:T(8,128)(2,1)} %param.15) | copy-start | bytes 294916
  7.2 6.9 %copy-start.12 = (bf16[2,8,8,1536]{3,2,1,0:T(8,128)(2,1)S(1)}, bf16[2,8,8,1536]{3,2,1,0:T(8,128)(2,1)}, u32[]{:S(2)}) copy-start(bf16[2,8,8,1536]{3,2,1,0:T(8,128)(2,1)} %param.12) | copy-start | bytes 1179652
  7.2 54.4 %all-reduce.7.cloned.1.call-start = ((), (), s32[]{:S(2)}) async-start(), calls=%async_computation | async-start | bytes 786432 | tf_op jit(solution)/shard_map/psum | solution.py:129
  7.2 7.7 %copy-start.13 = (bf16[32,1536]{1,0:T(8,128)(2,1)S(1)}, bf16[32,1536]{1,0:T(8,128)(2,1)}, u32[]{:S(2)}) copy-start(bf16[32,1536]{1,0:T(8,128)(2,1)} %param.16) | copy-start | bytes 294916
  8.4 9.9 %collective-permute-start = (bf16[2,2,2,8,1536]{4,3,2,1,0:T(8,128)(2,1)S(1)}, bf16[2,2,2,8,1536]{4,3,2,1,0:T(8,128)(2,1)S(1)}, u32[]{:S(2)}, u32[]{:S(2)}) collective-permute-start(bf16[2,2,2,8,1536]{4,3,2,1,0:T(8,128)(2,1)S(1)} %get-tuple-element.20), channel_id=1, source_target_pairs={{0,4},{4,8},{8,12},{12,0},{1,5},{5,9},{9,13},{13,1},{2,6},{6,10},{... | collective-permute-start | bytes 589832 | tf_op jit(solution)/shard_map/ppermute | solution.py:26
  9.0 9.3 %collective-permute-start.1 = (bf16[2,2,2,8,1536]{4,3,2,1,0:T(8,128)(2,1)S(1)}, bf16[2,2,2,8,1536]{4,3,2,1,0:T(8,128)(2,1)S(1)}, u32[]{:S(2)}, u32[]{:S(2)}) collective-permute-start(bf16[2,2,2,8,1536]{4,3,2,1,0:T(8,128)(2,1)S(1)} %get-tuple-element.21), channel_id=1, source_target_pairs={{4,0},{8,4},{12,8},{0,12},{5,1},{9,5},{13,9},{1,13},{6,2},{10,6},{... | collective-permute-start | bytes 589832 | tf_op jit(solution)/shard_map/ppermute | solution.py:28
  14.4 3.9 %copy-start.7 = (bf16[2,8,8,1536]{3,2,1,0:T(8,128)(2,1)S(1)}, bf16[2,8,8,1536]{3,2,1,0:T(8,128)(2,1)}, u32[]{:S(2)}) copy-start(bf16[2,8,8,1536]{3,2,1,0:T(8,128)(2,1)} %param.11) | copy-start | bytes 1179652
  14.4 3.9 %copy-start.8 = (bf16[2,8,8,1536]{3,2,1,0:T(8,128)(2,1)S(1)}, bf16[2,8,8,1536]{3,2,1,0:T(8,128)(2,1)}, u32[]{:S(2)}) copy-start(bf16[2,8,8,1536]{3,2,1,0:T(8,128)(2,1)} %param.10) | copy-start | bytes 1179652
  15.3 0.7 copy-start.9
  18.7 58.3 %collective-permute-start.2 = (bf16[2,2,12,2,1536]{4,3,2,1,0:T(2,128)(2,1)S(1)}, bf16[2,2,12,2,1536]{4,3,2,1,0:T(2,128)(2,1)S(1)}, u32[]{:S(2)}, u32[]{:S(2)}) collective-permute-start(bf16[2,2,12,2,1536]{4,3,2,1,0:T(2,128)(2,1)S(1)} %get-tuple-element.16), channel_id=1, source_target_pairs={{0,1},{1,2},{2,3},{3,0},{4,5},{5,6},{6,7},{7,4},{8,9},{9,10},{10,1... | collective-permute-start | bytes 884744 | tf_op jit(solution)/shard_map/ppermute | solution.py:26
  21.1 56.0 %collective-permute-start.3 = (bf16[2,2,12,2,1536]{4,3,2,1,0:T(2,128)(2,1)S(1)}, bf16[2,2,12,2,1536]{4,3,2,1,0:T(2,128)(2,1)S(1)}, u32[]{:S(2)}, u32[]{:S(2)}) collective-permute-start(bf16[2,2,12,2,1536]{4,3,2,1,0:T(2,128)(2,1)S(1)} %get-tuple-element.17), channel_id=1, source_target_pairs={{1,0},{2,1},{3,2},{0,3},{5,4},{6,5},{7,6},{4,7},{9,8},{10,9},{11,1... | collective-permute-start | bytes 884744 | tf_op jit(solution)/shard_map/ppermute | solution.py:28
  81.2 2.2 %copy-start.4 = (bf16[288,12,128]{2,1,0:T(8,128)(2,1)}, bf16[288,12,128]{2,1,0:T(8,128)(2,1)S(1)}, u32[]{:S(2)}) copy-start(bf16[288,12,128]{2,1,0:T(8,128)(2,1)S(1)} %reshape_squeeze.8) | copy-start | bytes 2654212
  81.8 1.6 %copy-start.6 = (bf16[288,12,128]{2,1,0:T(8,128)(2,1)S(1)}, bf16[288,12,128]{2,1,0:T(8,128)(2,1)}, u32[]{:S(2)}) copy-start(bf16[288,12,128]{2,1,0:T(8,128)(2,1)} %reshape_squeeze.9) | copy-start | bytes 2654212
  83.9 0.9 copy-start.2
  96.9 1.7 %copy-start.1 = (f32[1,2,12,12,1536]{4,3,2,1,0:T(8,128)S(1)}, f32[1,2,12,12,1536]{4,3,2,1,0:T(8,128)}, u32[]{:S(2)}) copy-start(f32[1,2,12,12,1536]{4,3,2,1,0:T(8,128)} %stack.31) | copy-start | bytes 5308420
  98.8 1.6 %copy-start.11 = (bf16[2,32,12,128]{3,1,2,0:T(8,128)(2,1)S(1)}, bf16[2,32,12,128]{3,1,2,0:T(8,128)(2,1)}, u32[]{:S(2)}) copy-start(bf16[2,32,12,128]{3,1,2,0:T(8,128)(2,1)} %all-reduce.8) | copy-start | bytes 589828
  99.9 12.6 %collective-permute-start.5 = (f32[2,2,2,12,1536]{4,2,3,1,0:T(2,128)S(1)}, f32[2,2,2,12,1536]{4,2,3,1,0:T(2,128)S(1)}, u32[]{:S(2)}, u32[]{:S(2)}) collective-permute-start(f32[2,2,2,12,1536]{4,2,3,1,0:T(2,128)S(1)} %copy.80), channel_id=1, source_target_pairs={{0,12},{4,0},{8,4},{12,8},{1,13},{5,1},{9,5},{13,9},{2,14},{6,2},{... | collective-permute-start | bytes 1769480 | tf_op jit(solution)/shard_map/ppermute | solution.py:16
  99.9 15.8 %collective-permute-start.4 = (f32[2,2,2,12,1536]{4,2,3,1,0:T(2,128)S(1)}, f32[2,2,2,12,1536]{4,2,3,1,0:T(2,128)S(1)}, u32[]{:S(2)}, u32[]{:S(2)}) collective-permute-start(f32[2,2,2,12,1536]{4,2,3,1,0:T(2,128)S(1)} %copy.78), channel_id=1, source_target_pairs={{0,4},{4,8},{8,12},{12,0},{1,5},{5,9},{9,13},{13,1},{2,6},{6,10},{... | collective-permute-start | bytes 1769480 | tf_op jit(solution)/shard_map/ppermute | solution.py:16
  115.9 5.5 %copy-start.3 = (bf16[12,288,128]{2,1,0:T(8,128)(2,1)S(1)}, bf16[12,288,128]{2,1,0:T(8,128)(2,1)}, u32[]{:S(2)}) copy-start(bf16[12,288,128]{2,1,0:T(8,128)(2,1)} %copy-done.2) | copy-start | bytes 2654212
  115.9 5.4 %copy-start.5 = (bf16[288,12,128]{2,1,0:T(8,128)(2,1)S(1)}, bf16[288,12,128]{2,1,0:T(8,128)(2,1)}, u32[]{:S(2)}) copy-start(bf16[288,12,128]{2,1,0:T(8,128)(2,1)} %copy-done.4) | copy-start | bytes 2654212
  116.3 5.6 %copy-start.10 = (bf16[12,128,32]{1,2,0:T(8,128)(2,1)S(1)}, bf16[12,128,32]{1,2,0:T(8,128)(2,1)}, u32[]{:S(2)}) copy-start(bf16[12,128,32]{1,2,0:T(8,128)(2,1)} %copy-done.9) | copy-start | bytes 294916
  117.5 14.1 %collective-permute-start.6 = (f32[2,2,8,2,1536]{4,3,2,1,0:T(2,128)}, f32[2,2,8,2,1536]{4,3,2,1,0:T(2,128)}, u32[]{:S(2)}, u32[]{:S(2)}) collective-permute-start(f32[2,2,8,2,1536]{4,3,2,1,0:T(2,128)} %get-tuple-element.12), channel_id=1, source_target_pairs={{0,1},{1,2},{2,3},{3,0},{4,5},{5,6},{6,7},{7,4},{8,9},{9,10},{10,1... | collective-permute-start | bytes 1179656 | tf_op jit(solution)/shard_map/ppermute | solution.py:16
  119.0 19.7 %collective-permute-start.7 = (f32[2,2,8,2,1536]{4,3,2,1,0:T(2,128)}, f32[2,2,8,2,1536]{4,3,2,1,0:T(2,128)}, u32[]{:S(2)}, u32[]{:S(2)}) collective-permute-start(f32[2,2,8,2,1536]{4,3,2,1,0:T(2,128)} %get-tuple-element.13), channel_id=1, source_target_pairs={{0,3},{1,0},{2,1},{3,2},{4,7},{5,4},{6,5},{7,6},{8,11},{9,8},{10,9... | collective-permute-start | bytes 1179656 | tf_op jit(solution)/shard_map/ppermute | solution.py:16
Sparse Core Ops, SparseCore 0:
  17.1 44.4 all-reduce.6
